TPU v7x, 32 devices: a 4x4x1 block of a 4x4x8 slice. The times are simulated.
32 devices in a mesh: dp: 1 (over z), ing: 4 (over y), grp: 8 (over x, core).
Axes of the slice: x: 4, y: 4, z: 1, core: 2. Of those that a mesh axis runs over, the one named last changes fastest.
The devices are a block of a 4x4x8 slice.
Arguments:
- x: bfloat16 [16384, 2048], P(('dp', 'grp', 'ing'))
- idx: int32 [16384, 3, 2], P(('dp', 'grp', 'ing'))
- g: float32 [16384, 3, 2], P(('dp', 'grp', 'ing'))
- w1: bfloat16 [64, 2048, 1408], P(('grp', 'ing'))
- w3: bfloat16 [64, 2048, 1408], P(('grp', 'ing'))
- w2: bfloat16 [64, 1408, 2048], P(('grp', 'ing'))
- s1: bfloat16 [2048, 2816], replicated
- s3: bfloat16 [2048, 2816], replicated
- s2: bfloat16 [2816, 2048], replicated
Outputs:
- output: bfloat16 [16384, 2048], P(('dp', 'grp', 'ing'))
All inputs are finite; a program needn't handle non-finite values.
Results may differ from a plain program's by a relative error of at most 0.00112.
Values are sent between devices in bfloat16 or wider.
A program may use at most 768 MiB of HBM per device.

v0:
```python
import functools

import jax
import jax.numpy as jnp
from jax import lax
from jax.experimental import pallas as pl
from jax.experimental.pallas import tpu as pltpu
from jax.sharding import PartitionSpec as P

MESH = pl.DeviceIdType.MESH
LANES = 128


def _moe_kernel(G, n, EL, C, CG, T, D, F, K,
                x_ref, it_ref, gt_ref, ic_ref, w1_ref, w3_ref, w2_ref, s1_ref, s3_ref, s2_ref,
                y_ref, pr, xg, xs, xr, es, er, ps,
                W1, W3, W2, xb, eb, rb, pb, fb, hb, xgv, selv, putv, wqv, acc, tri, cvec,
                icv, idxy, idxx, gx,
                agS, agR, iyS, iyR, ixS, ixR, gxS, gxR, xS, xR, eS, eR, pS, pR, lsem, wsem):
    EG = EL * n
    CB = EL * C
    R = n * CB
    RE = n * C
    M = K // 2
    H = T // 2
    NB = min(256, D)
    LAG = 4
    bf = jnp.bfloat16
    f32 = jnp.float32
    i32 = jnp.int32
    d = lax.axis_index('dp')
    j = lax.axis_index('ing')
    b = lax.axis_index('grp')
    chips = G // 2
    chip, core = b // 2, b % 2

    def grp_at(s):
        q, r = s // 2, s % 2
        mid = ((q + 1) // 2) % 2
        dc = mid * (1 + 2 * r) + (q // 3) * 2
        dcore = (1 - mid) * r + mid * (q - 1)
        return 2 * ((chip + dc) % chips) + (core + dcore) % 2

    def inv(s):
        q, r = s // 2, s % 2
        mid = ((q + 1) // 2) % 2
        return 2 * q + r + mid * (1 - 2 * r)

    def xdev(s):
        return (d, j, grp_at(s))

    def ydev(k):
        return (d, (j + k) % n, b)

    def iota(shape, dim):
        return lax.broadcasted_iota(i32, shape, dim)

    def remote(src, dst, ss, rs, dev):
        return pltpu.make_async_remote_copy(src_ref=src, dst_ref=dst, send_sem=ss, recv_sem=rs,
                                            device_id=dev, device_id_type=MESH)

    barrier = pltpu.get_barrier_semaphore()
    for k in range(1, n):
        pl.semaphore_signal(barrier, 1, device_id=ydev(k), device_id_type=MESH)
    for s in range(1, G):
        pl.semaphore_signal(barrier, 1, device_id=xdev(s), device_id_type=MESH)
    pl.semaphore_wait(barrier, n - 1 + G - 1)

    def ag(k):
        return remote(x_ref, xg.at[k], agS.at[k], agR.at[k], ydev(n - k))

    def fwd(h):
        k, dev = (1, n - 1) if h == 0 else (n - 1, 1)
        rows = pl.ds(h * H, H)
        return remote(xg.at[k, rows], xg.at[2, rows], agS.at[2 * h], agR.at[2 * h], ydev(dev))

    def iy(k):
        return remote(it_ref, idxy.at[k], iyS.at[k], iyR.at[k], ydev(n - k))

    def ix(s):
        return remote(it_ref, idxx.at[inv(s)], ixS.at[s], ixR.at[inv(s)], xdev(s))

    def ixrecv(s):
        return remote(it_ref, idxx.at[s], ixS.at[s], ixR.at[s], xdev(s))

    def gxc(s):
        return remote(gt_ref, gx.at[inv(s)], gxS.at[s], gxR.at[inv(s)], xdev(s))

    def gxrecv(s):
        return remote(gt_ref, gx.at[s], gxS.at[s], gxR.at[s], xdev(s))

    def xcopy(s, k):
        return remote(xs.at[k, grp_at(s)], xr.at[inv(s), k], xS.at[s, k], xR.at[inv(s), k], xdev(s))

    def xrecv(s, k):
        return remote(xs.at[k, grp_at(s)], xr.at[s, k], xS.at[s, k], xR.at[s, k], xdev(s))

    def ecopy(s, k):
        return remote(es.at[s, k], er.at[s, n - k], eS.at[s, k], eR.at[s, n - k], ydev(k))

    def erecv(s, k):
        return remote(es.at[s, k], er.at[s, k], eS.at[s, k], eR.at[s, k], ydev(k))

    def pcopy(s):
        return remote(ps.at[s], pr.at[b], pS.at[s], pR.at[b], xdev(s))

    def precv(s):
        g = grp_at(s)
        return remote(ps.at[s], pr.at[g], pS.at[s], pR.at[g], xdev(s))

    def run(copies):
        for c in copies:
            c.start()
        for c in copies:
            c.wait()

    for k in range(1, n):
        iy(k).start()
    ag(1).start()
    ag(n - 1).start()

    def weights(l, shared):
        cols = pl.ds(l * F, F)
        srcs = ((s1_ref.at[:, cols], s3_ref.at[:, cols], s2_ref.at[cols]) if shared
                else (w1_ref.at[l], w3_ref.at[l], w2_ref.at[l]))
        return [pltpu.make_async_copy(s, w.at[l], wsem.at[l, i])
                for i, (s, w) in enumerate(zip(srcs, (W1, W3, W2)))]

    run([pltpu.make_async_copy(it_ref, idxy.at[0], lsem.at[0]),
         pltpu.make_async_copy(it_ref, idxx.at[0], lsem.at[1]),
         pltpu.make_async_copy(gt_ref, gx.at[0], lsem.at[2]),
         pltpu.make_async_copy(ic_ref, icv, lsem.at[3]),
         pltpu.make_async_copy(x_ref, xgv, lsem.at[4])])
    for s in range(1, G):
        ix(s).start()
        gxc(s).start()
    for l in range(EL):
        for c in weights(l, True):
            c.start()
    tri[...] = (iota((T, T), 0) < iota((T, T), 1)).astype(f32).astype(bf)

    def one_hot_rows(iv, eid):
        oh = iv[0:1, :] == eid
        for i in range(1, K):
            oh = oh | (iv[i:i + 1, :] == eid)
        return oh

    def gather(k):
        iv = idxy[k]
        r = iota((G * EL, T), 0)
        g_of = jnp.zeros((G * EL, T), i32)
        for q in range(1, G):
            g_of = g_of + (r >= q * EL).astype(i32)
        eid = g_of * (EG - EL) + r + j * EL
        oh = one_hot_rows(iv, eid)
        rank = jnp.dot(oh.astype(f32).astype(bf), tri[...], preferred_element_type=f32)
        code = jnp.where(oh, rank.astype(i32), -(EL * C))
        row = iota((CB, T), 0)
        for g in range(G):
            want = code[g * EL:g * EL + 1, :]
            for l in range(1, EL):
                want = jnp.where(row < l * C, want, code[g * EL + l:g * EL + l + 1, :] + l * C)
            selv[g * CB:(g + 1) * CB, :] = (row == want).astype(f32).astype(bf)

        def col(i, _):
            cols = pl.ds(pl.multiple_of(i * NB, NB), NB)
            xb[:, cols] = jnp.dot(selv[...], xgv[:, cols], preferred_element_type=f32).astype(bf)
            return 0

        lax.fori_loop(0, D // NB, col, 0)
        run([pltpu.make_async_copy(xb.at[pl.ds(g * CB, CB)], xs.at[k, g], lsem.at[g]) for g in range(G)]
            + [pltpu.make_async_copy(xb.at[pl.ds(pl.multiple_of(b * CB, 8), CB)], xr.at[0, k], lsem.at[G])])

    def fetch(k):
        run([pltpu.make_async_copy(xg.at[k], xgv, lsem.at[0])])

    def up(l, src, rows, m):
        def body(i, _):
            cols = pl.ds(pl.multiple_of(i * LANES, LANES), LANES)
            w = jnp.concatenate([W1[l, :, cols], W3[l, :, cols]], axis=1)
            hh = jnp.dot(src[rows, :], w, preferred_element_type=f32)
            a, c = hh[:, :LANES], hh[:, LANES:]
            hb[0:m, cols] = (a * jax.nn.sigmoid(a) * c).astype(bf)
            return 0

        lax.fori_loop(0, F // LANES, body, 0)

    gather(0)
    for s in range(1, G):
        xcopy(s, 0).start()

    lane = iota((T, LANES), 1)
    hit = jnp.zeros((T, LANES), i32)
    for m in range(M):
        v = icv[:, 2 * m:2 * m + 1]
        hit = hit + ((v >= lane * EG) & (v < lane * EG + EG)).astype(i32)
    below = lax.dot_general(tri[...], hit.astype(f32).astype(bf), (((0,), (0,)), ((), ())),
                            preferred_element_type=f32)
    cvec[...] = jnp.where(hit > 0, below.astype(i32), -1)

    for l in range(EL):
        for c in weights(l, True):
            c.wait()
        up(l, xgv, pl.ds(0, T), T)

        def down(i, _):
            cols = pl.ds(pl.multiple_of(i * NB, NB), NB)
            t = jnp.dot(hb[...], W2[l, :, cols], preferred_element_type=f32)
            acc[:, cols] = t if l == 0 else acc[:, cols] + t
            return 0

        lax.fori_loop(0, D // NB, down, 0)
        for c in weights(l, False):
            c.start()

    for k in (1, n - 1):
        iy(k).wait_recv()
        ag(k).wait_recv()
        fwd(0 if k == 1 else 1).start()
        fetch(k)
        gather(k)
        for s in range(1, 6):
            xcopy(s, k).start()
    iy(2).wait_recv()
    fwd(0).wait_recv()
    fwd(1).wait_recv()
    fetch(2)
    gather(2)
    for s in range(1, 6):
        xcopy(s, 2).start()
    for s in range(6, G):
        for k in range(1, n):
            xcopy(s, k).start()
    for l in range(EL):
        for c in weights(l, False):
            c.wait()
    for s in range(1, G):
        ixrecv(s).wait_recv()
        gxrecv(s).wait_recv()

    def expert(s):
        @pl.when(s > 0)
        def _():
            for k in range(n):
                xrecv(s, k).wait_recv()
        run([pltpu.make_async_copy(xr.at[s, k, pl.ds(l * C, C)], xb.at[pl.ds(l * RE + k * C, C)],
                                   lsem.at[k * EL + l]) for k in range(n) for l in range(EL)])

        def one(l, _):
            rows = pl.ds(pl.multiple_of(l * RE, 8), RE)
            up(l, xb, rows, RE)

            def down(i, _):
                cols = pl.ds(pl.multiple_of(i * NB, NB), NB)
                eb[rows, cols] = jnp.dot(hb[0:RE, :], W2[l, :, cols], preferred_element_type=f32).astype(bf)
                return 0

            lax.fori_loop(0, D // NB, down, 0)
            return 0

        lax.fori_loop(0, EL, one, 0)
        run([pltpu.make_async_copy(eb.at[pl.ds(l * RE + k * C, C)],
                                   (er.at[s, 0] if k == 0 else es.at[s, k]).at[pl.ds(l * C, C)],
                                   lsem.at[k * EL + l]) for k in range(n) for l in range(EL)])
        for k in range(1, n):
            ecopy(s, k).start()

    def combine(s):
        iv, gv = idxx[s], gx[s]
        r = iota((2 * EG, T), 0)
        oh = one_hot_rows(iv, r + b * EG) & (r < EG)
        mine = [(iv[2 * m:2 * m + 1, :] >= b * EG) & (iv[2 * m:2 * m + 1, :] < b * EG + EG) for m in range(M)]
        hit = mine[0]
        for m in range(1, M):
            hit = hit | mine[m]
        ohf = jnp.where(r == EG, hit.astype(f32), oh.astype(f32))
        cnt = jnp.dot(ohf.astype(bf), tri[...], preferred_element_type=f32).astype(i32)
        slot = jnp.where(hit, cnt[EG:EG + 1, :], -1)
        jd = jnp.zeros((2 * EG, T), i32)
        for q in range(1, n):
            jd = jd + (r >= q * EL).astype(i32)
        kk = jd - j
        kk = jnp.where(kk < 0, kk + n, kk)
        place = kk * CB + (r - jd * EL) * C + cnt
        at = iota((CG, T), 0) == slot
        atb = at.astype(f32).astype(bf)
        for i in range(2):
            ei = jnp.zeros((1, T), i32)
            gi = jnp.zeros((1, T), f32)
            for m in range(M):
                ei = ei + jnp.where(mine[m], iv[2 * m + i:2 * m + i + 1, :], 0)
                gi = gi + jnp.where(mine[m], gv[2 * m + i:2 * m + i + 1, :], 0.0)
            row = jnp.sum(jnp.where((r + b * EG == ei) & (r < EG), place, 0), axis=0, keepdims=True)
            row = jnp.where(hit, row, -1)
            inrow = (iota((R, T), 0) == row).astype(f32).astype(bf)
            putv[i] = lax.dot_general(atb, inrow, (((1,), (1,)), ((), ())), preferred_element_type=f32).astype(bf)
            w = jnp.sum(jnp.where(at, gi, 0.0), axis=1, keepdims=True)
            wqv[i] = jnp.broadcast_to(w, (CG, LANES))
        for k in range(1, n):
            erecv(s, k).wait_recv()
        run([pltpu.make_async_copy(er.at[s, k], rb.at[pl.ds(k * CB, CB)], lsem.at[k]) for k in range(n)])

        def col(i, _):
            cols = pl.ds(pl.multiple_of(i * NB, NB), NB)
            t = jnp.zeros((CG, NB), f32)
            for h in range(2):
                got = jnp.dot(putv[h], rb[:, cols], preferred_element_type=f32)
                t = t + got * jnp.concatenate([wqv[h]] * (NB // LANES), axis=1)
            pb[:, cols] = t.astype(bf)
            return 0

        lax.fori_loop(0, D // NB, col, 0)

        @pl.when(s == 0)
        def _():
            run([pltpu.make_async_copy(pb, pr.at[b], lsem.at[0])])

        @pl.when(s > 0)
        def _():
            run([pltpu.make_async_copy(pb, ps.at[s], lsem.at[0])])
            pcopy(s).start()

    def final(s):
        @pl.when(s > 0)
        def _():
            precv(s).wait_recv()
        g = grp_at(s)
        run([pltpu.make_async_copy(pr.at[g], fb, lsem.at[0])])
        code = jnp.sum(jnp.where(iota((T, LANES), 1) == g, cvec[...], 0), axis=1, keepdims=True)
        at = (iota((T, CG), 1) == code).astype(f32).astype(bf)

        def col(i, _):
            cols = pl.ds(pl.multiple_of(i * NB, NB), NB)
            acc[:, cols] = acc[:, cols] + jnp.dot(at, fb[:, cols], preferred_element_type=f32)
            return 0

        lax.fori_loop(0, D // NB, col, 0)

    def step(s, _):
        @pl.when(s < G)
        def _():
            expert(s)

        @pl.when((s > 0) & (s <= G))
        def _():
            combine(s - 1)

        @pl.when(s >= LAG)
        def _():
            final(s - LAG)
        return 0

    lax.fori_loop(0, G + LAG, step, 0)

    def out(i, _):
        cols = pl.ds(pl.multiple_of(i * NB, NB), NB)
        xgv[:, cols] = acc[:, cols].astype(bf)
        return 0

    lax.fori_loop(0, D // NB, out, 0)
    run([pltpu.make_async_copy(xgv, y_ref, lsem.at[0])])

    for k in range(1, n):
        iy(k).wait_send()
    ag(1).wait_send()
    ag(n - 1).wait_send()
    fwd(0).wait_send()
    fwd(1).wait_send()
    for s in range(1, G):
        ix(s).wait_send()
        gxc(s).wait_send()
        for k in range(n):
            xcopy(s, k).wait_send()
        pcopy(s).wait_send()
    for s in range(G):
        for k in range(1, n):
            ecopy(s, k).wait_send()


def solution(mesh):
    G = mesh.shape['grp']
    n = mesh.shape['ing']
    tok = P(('dp', 'grp', 'ing'), None)
    tok3 = P(('dp', 'grp', 'ing'), None, None)
    exp = P(('grp', 'ing'), None, None)

    def local(x, idx, g, w1, w3, w2, s1, s3, s2):
        T, D = x.shape
        _, M, KG = idx.shape
        K = M * KG
        EL, _, F = w1.shape
        E = EL * G * n
        C = (3 * T * K + 2 * E - 1) // (2 * E)
        CG = min(T, 3 * T * M // (2 * G))
        CB = EL * C
        R = n * CB
        flat = idx.reshape(T, K)
        it = jnp.pad(flat.T, ((0, 8 - K), (0, 0)))
        gt = jnp.pad(g.reshape(T, K).T, ((0, 8 - K), (0, 0)))
        ic = jnp.pad(flat, ((0, 0), (0, LANES - K)))
        anyspec = pl.BlockSpec(memory_space=pl.ANY)
        bf, f32, i32 = jnp.bfloat16, jnp.float32, jnp.int32
        sds = jax.ShapeDtypeStruct
        dma = lambda *s: pltpu.SemaphoreType.DMA(s)
        out = pl.pallas_call(
            functools.partial(_moe_kernel, G, n, EL, C, CG, T, D, F, K),
            out_shape=[sds((T, D), bf), sds((G, CG, D), bf), sds((n, T, D), bf), sds((n, G, CB, D), bf),
                       sds((G, n, CB, D), bf), sds((G, n, CB, D), bf), sds((G, n, CB, D), bf),
                       sds((G, CG, D), bf)],
            in_specs=[anyspec] * 10,
            out_specs=[anyspec] * 8,
            scratch_shapes=[
                pltpu.VMEM((EL, D, F), bf), pltpu.VMEM((EL, D, F), bf), pltpu.VMEM((EL, F, D), bf),
                pltpu.VMEM((G * CB, D), bf), pltpu.VMEM((R, D), bf), pltpu.VMEM((R, D), bf),
                pltpu.VMEM((CG, D), bf), pltpu.VMEM((CG, D), bf), pltpu.VMEM((T, F), bf),
                pltpu.VMEM((T, D), bf), pltpu.VMEM((G * CB, T), bf),
                pltpu.VMEM((KG, CG, R), bf), pltpu.VMEM((KG, CG, LANES), f32),
                pltpu.VMEM((T, D), f32), pltpu.VMEM((T, T), bf), pltpu.VMEM((T, LANES), i32),
                pltpu.VMEM((T, LANES), i32), pltpu.VMEM((n, 8, T), i32), pltpu.VMEM((G, 8, T), i32),
                pltpu.VMEM((G, 8, T), f32),
                dma(n), dma(n), dma(n), dma(n), dma(G), dma(G), dma(G), dma(G),
                dma(G, n), dma(G, n), dma(G, n), dma(G, n), dma(G), dma(G), dma(G + n), dma(EL, 3),
            ],
            compiler_params=pltpu.CompilerParams(
                collective_id=0, has_side_effects=True, vmem_limit_bytes=63 * 1024 * 1024),
            name="moe",
        )(x, it, gt, ic, w1, w3, w2, s1, s3, s2)
        return out[0]

    return jax.shard_map(local, mesh=mesh, in_specs=(tok, tok3, tok3, exp, exp, exp, P(), P(), P()),
                         out_specs=tok, check_vma=False)
```

profile of v0, /device:TPU:101, one launch (start us, length us, event | category | flops | bytes accessed | tf_op | source)
XLA Modules:
  0.0 390.6 jit_solution(2247637775841671740)
XLA Ops:
  0.0 0.7 reshape.6
  0.7 0.6 pad.12.it_ref
  1.3 0.7 reshape.7
  2.0 0.6 pad.13.gt_ref
  2.6 0.1 copy.12
  2.8 0.7 pad.14.ic_ref
  3.5 383.9 %moe.1 = (bf16[512,2048]{1,0:T(8,128)(2,1)}, bf16[8,288,2048]{2,1,0:T(8,128)(2,1)}, bf16[4,512,2048]{2,1,0:T(8,128)(2,1)}, bf16[4,8,144,2048]{3,2,1,0:T(8,128)(2...) custom-call(bf16[512,2048]{1,0:T(8,128)(2,1)} %x_ref.1, ...), custom_call_target="tpu_custom_call" | custom-call | tf_op jit(solution)/shard_map/moe/pallas_call | solution.py:405
  387.4 3.2 copy.14
where the time goes:
time: 392 us; the launch traced here: 391 us
  Pallas kernels  384 us (98%)
  local copies, waits for them, and re-layouts  6.68 us (2%)
    pallas_call x1, Pallas kernels, local(): pl.pallas_call(functools.partial(_moe_kernel, G, n, EL, C, CG, T, D, F, K...  384 us

commit v1 on v0

--- a/solution.py
+++ b/solution.py
@@ -12,11 +12,11 @@
 
 
 def _moe_kernel(G, n, EL, C, CG, T, D, F, K,
-                x_ref, it_ref, gt_ref, ic_ref, w1_ref, w3_ref, w2_ref, s1_ref, s3_ref, s2_ref,
-                y_ref, pr, xg, xs, xr, es, er, ps,
+                x_ref, it_ref, gt_ref, w1_ref, w3_ref, w2_ref, s1_ref, s3_ref, s2_ref,
+                y_ref, pr, xg, xs, xr, er, ps,
                 W1, W3, W2, xb, eb, rb, pb, fb, hb, xgv, selv, putv, wqv, acc, tri, cvec,
-                icv, idxy, idxx, gx,
-                agS, agR, iyS, iyR, ixS, ixR, gxS, gxR, xS, xR, eS, eR, pS, pR, lsem, wsem):
+                idxy, idxx, gx,
+                agS, agR, iyS, iyR, ixS, ixR, gxS, gxR, xS, xR, eS, eR, pS, pR, oS, lsem, wsem, fsem):
     EG = EL * n
     CB = EL * C
     R = n * CB
@@ -24,7 +24,8 @@
     M = K // 2
     H = T // 2
     NB = min(256, D)
-    LAG = 4
+    LAG = 5
+    SELF = G - 1
     bf = jnp.bfloat16
     f32 = jnp.float32
     i32 = jnp.int32
@@ -35,16 +36,14 @@
     chip, core = b // 2, b % 2
 
     def grp_at(s):
-        q, r = s // 2, s % 2
-        mid = ((q + 1) // 2) % 2
-        dc = mid * (1 + 2 * r) + (q // 3) * 2
-        dcore = (1 - mid) * r + mid * (q - 1)
+        t = s - (s // 4) * (2 * s - 7)
+        dc = (t * (t + 1) // 2) % 4
+        dcore = (s // 4 + 1 - (s % 7 + 6) // 7) % 2
         return 2 * ((chip + dc) % chips) + (core + dcore) % 2
 
     def inv(s):
-        q, r = s // 2, s % 2
-        mid = ((q + 1) // 2) % 2
-        return 2 * q + r + mid * (1 - 2 * r)
+        u = s % 4
+        return s + (((u + 1) // 2) % 2) * (3 - 2 * u)
 
     def xdev(s):
         return (d, j, grp_at(s))
@@ -62,7 +61,7 @@
     barrier = pltpu.get_barrier_semaphore()
     for k in range(1, n):
         pl.semaphore_signal(barrier, 1, device_id=ydev(k), device_id_type=MESH)
-    for s in range(1, G):
+    for s in range(SELF):
         pl.semaphore_signal(barrier, 1, device_id=xdev(s), device_id_type=MESH)
     pl.semaphore_wait(barrier, n - 1 + G - 1)
 
@@ -95,11 +94,22 @@
     def xrecv(s, k):
         return remote(xs.at[k, grp_at(s)], xr.at[s, k], xS.at[s, k], xR.at[s, k], xdev(s))
 
-    def ecopy(s, k):
-        return remote(es.at[s, k], er.at[s, n - k], eS.at[s, k], eR.at[s, n - k], ydev(k))
-
-    def erecv(s, k):
-        return remote(es.at[s, k], er.at[s, k], eS.at[s, k], eR.at[s, k], ydev(k))
+    def erows(l, k):
+        return pl.ds(pl.multiple_of(l * RE + k * C, 8), C)
+
+    def lrows(l):
+        return pl.ds(pl.multiple_of(l * C, 8), C)
+
+    def ecopy(s, k, l):
+        return remote(eb.at[s % 2, erows(l, k)], er.at[s, n - k, lrows(l)],
+                      eS.at[s, l * n + k], eR.at[s, l * n + n - k], ydev(k))
+
+    def erecv(s, k, l):
+        return remote(eb.at[s % 2, erows(l, k)], er.at[s, k, lrows(l)],
+                      eS.at[s, l * n + k], eR.at[s, l * n + k], ydev(k))
+
+    def eown(s, l):
+        return pltpu.make_async_copy(eb.at[s % 2, erows(l, 0)], er.at[s, 0, lrows(l)], oS.at[s, l])
 
     def pcopy(s):
         return remote(ps.at[s], pr.at[b], pS.at[s], pR.at[b], xdev(s))
@@ -127,11 +137,10 @@
                 for i, (s, w) in enumerate(zip(srcs, (W1, W3, W2)))]
 
     run([pltpu.make_async_copy(it_ref, idxy.at[0], lsem.at[0]),
-         pltpu.make_async_copy(it_ref, idxx.at[0], lsem.at[1]),
-         pltpu.make_async_copy(gt_ref, gx.at[0], lsem.at[2]),
-         pltpu.make_async_copy(ic_ref, icv, lsem.at[3]),
+         pltpu.make_async_copy(it_ref, idxx.at[SELF], lsem.at[1]),
+         pltpu.make_async_copy(gt_ref, gx.at[SELF], lsem.at[2]),
          pltpu.make_async_copy(x_ref, xgv, lsem.at[4])])
-    for s in range(1, G):
+    for s in range(SELF):
         ix(s).start()
         gxc(s).start()
     for l in range(EL):
@@ -169,7 +178,7 @@
 
         lax.fori_loop(0, D // NB, col, 0)
         run([pltpu.make_async_copy(xb.at[pl.ds(g * CB, CB)], xs.at[k, g], lsem.at[g]) for g in range(G)]
-            + [pltpu.make_async_copy(xb.at[pl.ds(pl.multiple_of(b * CB, 8), CB)], xr.at[0, k], lsem.at[G])])
+            + [pltpu.make_async_copy(xb.at[pl.ds(pl.multiple_of(b * CB, 8), CB)], xr.at[SELF, k], lsem.at[G])])
 
     def fetch(k):
         run([pltpu.make_async_copy(xg.at[k], xgv, lsem.at[0])])
@@ -186,17 +195,18 @@
         lax.fori_loop(0, F // LANES, body, 0)
 
     gather(0)
-    for s in range(1, G):
+    for s in (1, 2, 5, 6, 3, 4, 0):
         xcopy(s, 0).start()
 
-    lane = iota((T, LANES), 1)
-    hit = jnp.zeros((T, LANES), i32)
+    iv = idxy[0]
+    gid = iota((2 * G, T), 0) * EG
+    hit = jnp.zeros((2 * G, T), i32)
     for m in range(M):
-        v = icv[:, 2 * m:2 * m + 1]
-        hit = hit + ((v >= lane * EG) & (v < lane * EG + EG)).astype(i32)
-    below = lax.dot_general(tri[...], hit.astype(f32).astype(bf), (((0,), (0,)), ((), ())),
-                            preferred_element_type=f32)
-    cvec[...] = jnp.where(hit > 0, below.astype(i32), -1)
+        v = iv[2 * m:2 * m + 1, :]
+        hit = hit + ((v >= gid) & (v < gid + EG)).astype(i32)
+    below = jnp.dot(hit.astype(f32).astype(bf), tri[...], preferred_element_type=f32)
+    code = jnp.where(hit > 0, below, -1.0)
+    cvec[...] = jnp.concatenate([code, jnp.zeros((LANES - 2 * G, T), f32)], axis=0).T
 
     for l in range(EL):
         for c in weights(l, True):
@@ -219,51 +229,62 @@
         fwd(0 if k == 1 else 1).start()
         fetch(k)
         gather(k)
-        for s in range(1, 6):
+        for s in range(3):
             xcopy(s, k).start()
     iy(2).wait_recv()
     fwd(0).wait_recv()
     fwd(1).wait_recv()
     fetch(2)
     gather(2)
-    for s in range(1, 6):
+    for s in range(3):
         xcopy(s, 2).start()
-    for s in range(6, G):
+    for s in range(3, SELF):
         for k in range(1, n):
             xcopy(s, k).start()
     for l in range(EL):
         for c in weights(l, False):
             c.wait()
-    for s in range(1, G):
+    for s in range(SELF):
         ixrecv(s).wait_recv()
         gxrecv(s).wait_recv()
 
     def expert(s):
-        @pl.when(s > 0)
+        @pl.when(s < SELF)
         def _():
             for k in range(n):
                 xrecv(s, k).wait_recv()
-        run([pltpu.make_async_copy(xr.at[s, k, pl.ds(l * C, C)], xb.at[pl.ds(l * RE + k * C, C)],
-                                   lsem.at[k * EL + l]) for k in range(n) for l in range(EL)])
+
+        def load(l, k):
+            return pltpu.make_async_copy(xr.at[s, k, lrows(l)], xb.at[erows(l, k)], lsem.at[l * n + k])
+
+        for l in range(EL):
+            for k in range(n):
+                load(l, k).start()
+
+        @pl.when(s >= 2)
+        def _():
+            for l in range(EL):
+                for k in range(1, n):
+                    ecopy(s - 2, k, l).wait_send()
 
         def one(l, _):
+            for k in range(n):
+                load(l, k).wait()
             rows = pl.ds(pl.multiple_of(l * RE, 8), RE)
             up(l, xb, rows, RE)
 
             def down(i, _):
                 cols = pl.ds(pl.multiple_of(i * NB, NB), NB)
-                eb[rows, cols] = jnp.dot(hb[0:RE, :], W2[l, :, cols], preferred_element_type=f32).astype(bf)
+                eb[s % 2, rows, cols] = jnp.dot(hb[0:RE, :], W2[l, :, cols], preferred_element_type=f32).astype(bf)
                 return 0
 
             lax.fori_loop(0, D // NB, down, 0)
+            for k in (1, n - 1, 2):
+                ecopy(s, k, l).start()
+            eown(s, l).start()
             return 0
 
         lax.fori_loop(0, EL, one, 0)
-        run([pltpu.make_async_copy(eb.at[pl.ds(l * RE + k * C, C)],
-                                   (er.at[s, 0] if k == 0 else es.at[s, k]).at[pl.ds(l * C, C)],
-                                   lsem.at[k * EL + l]) for k in range(n) for l in range(EL)])
-        for k in range(1, n):
-            ecopy(s, k).start()
 
     def combine(s):
         iv, gv = idxx[s], gx[s]
@@ -296,9 +317,16 @@
             putv[i] = lax.dot_general(atb, inrow, (((1,), (1,)), ((), ())), preferred_element_type=f32).astype(bf)
             w = jnp.sum(jnp.where(at, gi, 0.0), axis=1, keepdims=True)
             wqv[i] = jnp.broadcast_to(w, (CG, LANES))
-        for k in range(1, n):
-            erecv(s, k).wait_recv()
-        run([pltpu.make_async_copy(er.at[s, k], rb.at[pl.ds(k * CB, CB)], lsem.at[k]) for k in range(n)])
+        loads = [pltpu.make_async_copy(er.at[s, k], rb.at[pl.ds(k * CB, CB)], lsem.at[k]) for k in range(n)]
+        for l in range(EL):
+            eown(s, l).wait()
+        loads[0].start()
+        for k in (1, n - 1, 2):
+            for l in range(EL):
+                erecv(s, k, l).wait_recv()
+            loads[k].start()
+        for c in loads:
+            c.wait()
 
         def col(i, _):
             cols = pl.ds(pl.multiple_of(i * NB, NB), NB)
@@ -311,23 +339,32 @@
 
         lax.fori_loop(0, D // NB, col, 0)
 
-        @pl.when(s == 0)
-        def _():
-            run([pltpu.make_async_copy(pb, pr.at[b], lsem.at[0])])
-
-        @pl.when(s > 0)
-        def _():
-            run([pltpu.make_async_copy(pb, ps.at[s], lsem.at[0])])
+        @pl.when(s == SELF)
+        def _():
+            pltpu.make_async_copy(pb, pr.at[b], lsem.at[0]).start()
+
+        @pl.when(s < SELF)
+        def _():
+            pltpu.make_async_copy(pb, ps.at[s], lsem.at[0]).start()
+
+    def send_back(s):
+        pltpu.make_async_copy(pb, ps.at[s], lsem.at[0]).wait()
+
+        @pl.when(s < SELF)
+        def _():
             pcopy(s).start()
 
+    def final_load(s):
+        @pl.when(s < SELF)
+        def _():
+            precv(s).wait_recv()
+        pltpu.make_async_copy(pr.at[grp_at(s)], fb, fsem.at[0]).start()
+
     def final(s):
-        @pl.when(s > 0)
-        def _():
-            precv(s).wait_recv()
         g = grp_at(s)
-        run([pltpu.make_async_copy(pr.at[g], fb, lsem.at[0])])
-        code = jnp.sum(jnp.where(iota((T, LANES), 1) == g, cvec[...], 0), axis=1, keepdims=True)
-        at = (iota((T, CG), 1) == code).astype(f32).astype(bf)
+        pltpu.make_async_copy(pr.at[g], fb, fsem.at[0]).wait()
+        code = jnp.sum(jnp.where(iota((T, LANES), 1) == g, cvec[...], 0.0), axis=1, keepdims=True)
+        at = (iota((T, CG), 1) == code.astype(i32)).astype(f32).astype(bf)
 
         def col(i, _):
             cols = pl.ds(pl.multiple_of(i * NB, NB), NB)
@@ -344,6 +381,14 @@
         @pl.when((s > 0) & (s <= G))
         def _():
             combine(s - 1)
+
+        @pl.when(s >= LAG)
+        def _():
+            final_load(s - LAG)
+
+        @pl.when((s > 0) & (s <= G))
+        def _():
+            send_back(s - 1)
 
         @pl.when(s >= LAG)
         def _():
@@ -366,15 +411,16 @@
     ag(n - 1).wait_send()
     fwd(0).wait_send()
     fwd(1).wait_send()
-    for s in range(1, G):
+    for s in range(SELF):
         ix(s).wait_send()
         gxc(s).wait_send()
         for k in range(n):
             xcopy(s, k).wait_send()
         pcopy(s).wait_send()
-    for s in range(G):
-        for k in range(1, n):
-            ecopy(s, k).wait_send()
+    for s in range(G - 2, G):
+        for l in range(EL):
+            for k in range(1, n):
+                ecopy(s, k, l).wait_send()
 
 
 def solution(mesh):
@@ -395,9 +441,8 @@
         CB = EL * C
         R = n * CB
         flat = idx.reshape(T, K)
-        it = jnp.pad(flat.T, ((0, 8 - K), (0, 0)))
-        gt = jnp.pad(g.reshape(T, K).T, ((0, 8 - K), (0, 0)))
-        ic = jnp.pad(flat, ((0, 0), (0, LANES - K)))
+        it = flat.T
+        gt = g.reshape(T, K).T
         anyspec = pl.BlockSpec(memory_space=pl.ANY)
         bf, f32, i32 = jnp.bfloat16, jnp.float32, jnp.int32
         sds = jax.ShapeDtypeStruct
@@ -405,26 +450,26 @@
         out = pl.pallas_call(
             functools.partial(_moe_kernel, G, n, EL, C, CG, T, D, F, K),
             out_shape=[sds((T, D), bf), sds((G, CG, D), bf), sds((n, T, D), bf), sds((n, G, CB, D), bf),
-                       sds((G, n, CB, D), bf), sds((G, n, CB, D), bf), sds((G, n, CB, D), bf),
+                       sds((G, n, CB, D), bf), sds((G, n, CB, D), bf),
                        sds((G, CG, D), bf)],
-            in_specs=[anyspec] * 10,
-            out_specs=[anyspec] * 8,
+            in_specs=[anyspec] * 9,
+            out_specs=[anyspec] * 7,
             scratch_shapes=[
                 pltpu.VMEM((EL, D, F), bf), pltpu.VMEM((EL, D, F), bf), pltpu.VMEM((EL, F, D), bf),
-                pltpu.VMEM((G * CB, D), bf), pltpu.VMEM((R, D), bf), pltpu.VMEM((R, D), bf),
+                pltpu.VMEM((G * CB, D), bf), pltpu.VMEM((2, R, D), bf), pltpu.VMEM((R, D), bf),
                 pltpu.VMEM((CG, D), bf), pltpu.VMEM((CG, D), bf), pltpu.VMEM((T, F), bf),
                 pltpu.VMEM((T, D), bf), pltpu.VMEM((G * CB, T), bf),
                 pltpu.VMEM((KG, CG, R), bf), pltpu.VMEM((KG, CG, LANES), f32),
-                pltpu.VMEM((T, D), f32), pltpu.VMEM((T, T), bf), pltpu.VMEM((T, LANES), i32),
-                pltpu.VMEM((T, LANES), i32), pltpu.VMEM((n, 8, T), i32), pltpu.VMEM((G, 8, T), i32),
-                pltpu.VMEM((G, 8, T), f32),
+                pltpu.VMEM((T, D), f32), pltpu.VMEM((T, T), bf), pltpu.VMEM((T, LANES), f32),
+                pltpu.VMEM((n, K, T), i32), pltpu.VMEM((G, K, T), i32), pltpu.VMEM((G, K, T), f32),
                 dma(n), dma(n), dma(n), dma(n), dma(G), dma(G), dma(G), dma(G),
-                dma(G, n), dma(G, n), dma(G, n), dma(G, n), dma(G), dma(G), dma(G + n), dma(EL, 3),
+                dma(G, n), dma(G, n), dma(G, EL * n), dma(G, EL * n), dma(G), dma(G), dma(G, EL),
+                dma(G + n), dma(EL, 3), dma(1),
             ],
             compiler_params=pltpu.CompilerParams(
                 collective_id=0, has_side_effects=True, vmem_limit_bytes=63 * 1024 * 1024),
             name="moe",
-        )(x, it, gt, ic, w1, w3, w2, s1, s3, s2)
+        )(x, it, gt, w1, w3, w2, s1, s3, s2)
         return out[0]
 
     return jax.shard_map(local, mesh=mesh, in_specs=(tok, tok3, tok3, exp, exp, exp, P(), P(), P()),

time: 392 us -> 410 us (1.046)
  the two profiles are of different devices: /device:TPU:101 before, /device:TPU:98 now
where the time goes in v1:
time: 410 us; the launch traced here: 409 us
  Pallas kernels  403 us (98%)
  local copies, waits for them, and re-layouts  5.8 us (1%)
    pallas_call x1, Pallas kernels, local(): pl.pallas_call(functools.partial(_moe_kernel, G, n, EL, C, CG, T, D, F, K...  403 us

profile of v1, /device:TPU:98, one launch (start us, length us, event | category | flops | bytes accessed | tf_op | source)
XLA Modules:
  0.0 409.2 jit_solution(606293166145243862)
XLA Ops:
  0.0 1.3 reshape.6
  1.3 1.3 reshape.7
  2.6 403.4 %moe.1 = (bf16[512,2048]{1,0:T(8,128)(2,1)}, bf16[8,288,2048]{2,1,0:T(8,128)(2,1)}, bf16[4,512,2048]{2,1,0:T(8,128)(2,1)}, bf16[4,8,144,2048]{3,2,1,0:T(8,128)(2...) custom-call(bf16[512,2048]{1,0:T(8,128)(2,1)} %x_ref.1, ...), custom_call_target="tpu_custom_call" | custom-call | tf_op jit(solution)/shard_map/moe/pallas_call | solution.py:450
  406.1 3.2 copy.11

commit v2 on v1

--- a/solution.py
+++ b/solution.py
@@ -23,7 +23,7 @@
     RE = n * C
     M = K // 2
     H = T // 2
-    NB = min(256, D)
+    NB = min(512, D)
     LAG = 5
     SELF = G - 1
     bf = jnp.bfloat16
@@ -176,7 +176,7 @@
             xb[:, cols] = jnp.dot(selv[...], xgv[:, cols], preferred_element_type=f32).astype(bf)
             return 0
 
-        lax.fori_loop(0, D // NB, col, 0)
+        lax.fori_loop(0, D // NB, col, 0, unroll=True)
         run([pltpu.make_async_copy(xb.at[pl.ds(g * CB, CB)], xs.at[k, g], lsem.at[g]) for g in range(G)]
             + [pltpu.make_async_copy(xb.at[pl.ds(pl.multiple_of(b * CB, 8), CB)], xr.at[SELF, k], lsem.at[G])])
 
@@ -192,7 +192,7 @@
             hb[0:m, cols] = (a * jax.nn.sigmoid(a) * c).astype(bf)
             return 0
 
-        lax.fori_loop(0, F // LANES, body, 0)
+        lax.fori_loop(0, F // LANES, body, 0, unroll=True)
 
     gather(0)
     for s in (1, 2, 5, 6, 3, 4, 0):
@@ -219,7 +219,7 @@
             acc[:, cols] = t if l == 0 else acc[:, cols] + t
             return 0
 
-        lax.fori_loop(0, D // NB, down, 0)
+        lax.fori_loop(0, D // NB, down, 0, unroll=True)
         for c in weights(l, False):
             c.start()
 
@@ -229,16 +229,16 @@
         fwd(0 if k == 1 else 1).start()
         fetch(k)
         gather(k)
-        for s in range(3):
+        for s in (0, 1, 2, 3):
             xcopy(s, k).start()
     iy(2).wait_recv()
     fwd(0).wait_recv()
     fwd(1).wait_recv()
     fetch(2)
     gather(2)
-    for s in range(3):
+    for s in range(4):
         xcopy(s, 2).start()
-    for s in range(3, SELF):
+    for s in range(4, SELF):
         for k in range(1, n):
             xcopy(s, k).start()
     for l in range(EL):
@@ -278,7 +278,7 @@
                 eb[s % 2, rows, cols] = jnp.dot(hb[0:RE, :], W2[l, :, cols], preferred_element_type=f32).astype(bf)
                 return 0
 
-            lax.fori_loop(0, D // NB, down, 0)
+            lax.fori_loop(0, D // NB, down, 0, unroll=True)
             for k in (1, n - 1, 2):
                 ecopy(s, k, l).start()
             eown(s, l).start()
@@ -337,7 +337,7 @@
             pb[:, cols] = t.astype(bf)
             return 0
 
-        lax.fori_loop(0, D // NB, col, 0)
+        lax.fori_loop(0, D // NB, col, 0, unroll=True)
 
         @pl.when(s == SELF)
         def _():
@@ -371,7 +371,7 @@
             acc[:, cols] = acc[:, cols] + jnp.dot(at, fb[:, cols], preferred_element_type=f32)
             return 0
 
-        lax.fori_loop(0, D // NB, col, 0)
+        lax.fori_loop(0, D // NB, col, 0, unroll=True)
 
     def step(s, _):
         @pl.when(s < G)

time: 410 us -> 345 us (0.84)
  Pallas kernels: 403 us -> 338 us
    pallas_call x1, Pallas kernels: 403 us -> 338 us  [local(): pl.pallas_call(functools.partial(_moe_kernel, G, n, EL, C, CG, T, D, F, K...]
where the time goes in v2:
time: 345 us; the launch traced here: 344 us
  Pallas kernels  338 us (98%)
  local copies, waits for them, and re-layouts  5.8 us (2%)
    pallas_call x1, Pallas kernels, local(): pl.pallas_call(functools.partial(_moe_kernel, G, n, EL, C, CG, T, D, F, K...  338 us

profile of v2, /device:TPU:98, one launch (start us, length us, event | category | flops | bytes accessed | tf_op | source)
XLA Modules:
  0.0 343.5 jit_solution(6795069139209135346)
XLA Ops:
  0.0 1.3 reshape.6
  1.3 1.3 reshape.7
  2.6 337.7 %moe.1 = (bf16[512,2048]{1,0:T(8,128)(2,1)}, bf16[8,288,2048]{2,1,0:T(8,128)(2,1)}, bf16[4,512,2048]{2,1,0:T(8,128)(2,1)}, bf16[4,8,144,2048]{3,2,1,0:T(8,128)(2...) custom-call(bf16[512,2048]{1,0:T(8,128)(2,1)} %x_ref.1, ...), custom_call_target="tpu_custom_call" | custom-call | tf_op jit(solution)/shard_map/moe/pallas_call | solution.py:450
  340.4 3.2 copy.11

commit v3 on v2

--- a/solution.py
+++ b/solution.py
@@ -15,7 +15,7 @@
                 x_ref, it_ref, gt_ref, w1_ref, w3_ref, w2_ref, s1_ref, s3_ref, s2_ref,
                 y_ref, pr, xg, xs, xr, er, ps,
                 W1, W3, W2, xb, eb, rb, pb, fb, hb, xgv, selv, putv, wqv, acc, tri, cvec,
-                idxy, idxx, gx,
+                code, idxy, idxx, gx,
                 agS, agR, iyS, iyR, ixS, ixR, gxS, gxR, xS, xR, eS, eR, pS, pR, oS, lsem, wsem, fsem):
     EG = EL * n
     CB = EL * C
@@ -24,7 +24,7 @@
     M = K // 2
     H = T // 2
     NB = min(512, D)
-    LAG = 5
+    LAG = 4
     SELF = G - 1
     bf = jnp.bfloat16
     f32 = jnp.float32
@@ -89,10 +89,10 @@
         return remote(gt_ref, gx.at[s], gxS.at[s], gxR.at[s], xdev(s))
 
     def xcopy(s, k):
-        return remote(xs.at[k, grp_at(s)], xr.at[inv(s), k], xS.at[s, k], xR.at[inv(s), k], xdev(s))
+        return remote(xs.at[k, s], xr.at[inv(s), k], xS.at[s, k], xR.at[inv(s), k], xdev(s))
 
     def xrecv(s, k):
-        return remote(xs.at[k, grp_at(s)], xr.at[s, k], xS.at[s, k], xR.at[s, k], xdev(s))
+        return remote(xs.at[k, s], xr.at[s, k], xS.at[s, k], xR.at[s, k], xdev(s))
 
     def erows(l, k):
         return pl.ds(pl.multiple_of(l * RE + k * C, 8), C)
@@ -154,7 +154,7 @@
             oh = oh | (iv[i:i + 1, :] == eid)
         return oh
 
-    def gather(k):
+    def gather(k, first, second):
         iv = idxy[k]
         r = iota((G * EL, T), 0)
         g_of = jnp.zeros((G * EL, T), i32)
@@ -163,22 +163,37 @@
         eid = g_of * (EG - EL) + r + j * EL
         oh = one_hot_rows(iv, eid)
         rank = jnp.dot(oh.astype(f32).astype(bf), tri[...], preferred_element_type=f32)
-        code = jnp.where(oh, rank.astype(i32), -(EL * C))
+        code[...] = jnp.where(oh, rank.astype(i32), -(EL * C))
         row = iota((CB, T), 0)
-        for g in range(G):
-            want = code[g * EL:g * EL + 1, :]
-            for l in range(1, EL):
-                want = jnp.where(row < l * C, want, code[g * EL + l:g * EL + l + 1, :] + l * C)
-            selv[g * CB:(g + 1) * CB, :] = (row == want).astype(f32).astype(bf)
-
-        def col(i, _):
-            cols = pl.ds(pl.multiple_of(i * NB, NB), NB)
-            xb[:, cols] = jnp.dot(selv[...], xgv[:, cols], preferred_element_type=f32).astype(bf)
-            return 0
-
-        lax.fori_loop(0, D // NB, col, 0, unroll=True)
-        run([pltpu.make_async_copy(xb.at[pl.ds(g * CB, CB)], xs.at[k, g], lsem.at[g]) for g in range(G)]
-            + [pltpu.make_async_copy(xb.at[pl.ds(pl.multiple_of(b * CB, 8), CB)], xr.at[SELF, k], lsem.at[G])])
+        half = G // 2
+        outs = [pltpu.make_async_copy(xb.at[pl.ds(s * CB, CB)], xr.at[SELF, k] if s == SELF else xs.at[k, s],
+                                      lsem.at[s]) for s in range(G)]
+        for h in range(2):
+            for s in range(h * half, (h + 1) * half):
+                base = grp_at(s) * EL
+                want = code[pl.ds(base, 1), :]
+                for l in range(1, EL):
+                    want = jnp.where(row < l * C, want, code[pl.ds(base + l, 1), :] + l * C)
+                selv[s * CB:(s + 1) * CB, :] = (row == want).astype(f32).astype(bf)
+            if h == 1:
+                for c in outs[:half]:
+                    c.wait()
+                for s in first:
+                    xcopy(s, k).start()
+            rows = pl.ds(h * half * CB, half * CB)
+
+            def col(i, _):
+                cols = pl.ds(pl.multiple_of(i * NB, NB), NB)
+                xb[rows, cols] = jnp.dot(selv[rows, :], xgv[:, cols], preferred_element_type=f32).astype(bf)
+                return 0
+
+            lax.fori_loop(0, D // NB, col, 0, unroll=True)
+            for c in outs[h * half:(h + 1) * half]:
+                c.start()
+        for c in outs[half:]:
+            c.wait()
+        for s in second:
+            xcopy(s, k).start()
 
     def fetch(k):
         run([pltpu.make_async_copy(xg.at[k], xgv, lsem.at[0])])
@@ -194,9 +209,7 @@
 
         lax.fori_loop(0, F // LANES, body, 0, unroll=True)
 
-    gather(0)
-    for s in (1, 2, 5, 6, 3, 4, 0):
-        xcopy(s, 0).start()
+    gather(0, (1, 2, 3, 0), (5, 6, 4))
 
     iv = idxy[0]
     gid = iota((2 * G, T), 0) * EG
@@ -205,8 +218,8 @@
         v = iv[2 * m:2 * m + 1, :]
         hit = hit + ((v >= gid) & (v < gid + EG)).astype(i32)
     below = jnp.dot(hit.astype(f32).astype(bf), tri[...], preferred_element_type=f32)
-    code = jnp.where(hit > 0, below, -1.0)
-    cvec[...] = jnp.concatenate([code, jnp.zeros((LANES - 2 * G, T), f32)], axis=0).T
+    place = jnp.where(hit > 0, below, -1.0)
+    cvec[...] = jnp.concatenate([place, jnp.zeros((LANES - 2 * G, T), f32)], axis=0).T
 
     for l in range(EL):
         for c in weights(l, True):
@@ -228,16 +241,12 @@
         ag(k).wait_recv()
         fwd(0 if k == 1 else 1).start()
         fetch(k)
-        gather(k)
-        for s in (0, 1, 2, 3):
-            xcopy(s, k).start()
+        gather(k, (0, 1, 2, 3), ())
     iy(2).wait_recv()
     fwd(0).wait_recv()
     fwd(1).wait_recv()
     fetch(2)
-    gather(2)
-    for s in range(4):
-        xcopy(s, 2).start()
+    gather(2, (0, 1, 2, 3), ())
     for s in range(4, SELF):
         for k in range(1, n):
             xcopy(s, k).start()
@@ -363,8 +372,8 @@
     def final(s):
         g = grp_at(s)
         pltpu.make_async_copy(pr.at[g], fb, fsem.at[0]).wait()
-        code = jnp.sum(jnp.where(iota((T, LANES), 1) == g, cvec[...], 0.0), axis=1, keepdims=True)
-        at = (iota((T, CG), 1) == code.astype(i32)).astype(f32).astype(bf)
+        own = jnp.sum(jnp.where(iota((T, LANES), 1) == g, cvec[...], 0.0), axis=1, keepdims=True)
+        at = (iota((T, CG), 1) == own.astype(i32)).astype(f32).astype(bf)
 
         def col(i, _):
             cols = pl.ds(pl.multiple_of(i * NB, NB), NB)
@@ -373,6 +382,9 @@
 
         lax.fori_loop(0, D // NB, col, 0, unroll=True)
 
+    def turn(f):
+        return f + (f // 5) * (2 - 3 * ((f - 4) // 2))
+
     def step(s, _):
         @pl.when(s < G)
         def _():
@@ -384,7 +396,7 @@
 
         @pl.when(s >= LAG)
         def _():
-            final_load(s - LAG)
+            final_load(turn(s - LAG))
 
         @pl.when((s > 0) & (s <= G))
         def _():
@@ -392,7 +404,7 @@
 
         @pl.when(s >= LAG)
         def _():
-            final(s - LAG)
+            final(turn(s - LAG))
         return 0
 
     lax.fori_loop(0, G + LAG, step, 0)
@@ -461,7 +473,7 @@
                 pltpu.VMEM((T, D), bf), pltpu.VMEM((G * CB, T), bf),
                 pltpu.VMEM((KG, CG, R), bf), pltpu.VMEM((KG, CG, LANES), f32),
                 pltpu.VMEM((T, D), f32), pltpu.VMEM((T, T), bf), pltpu.VMEM((T, LANES), f32),
-                pltpu.VMEM((n, K, T), i32), pltpu.VMEM((G, K, T), i32), pltpu.VMEM((G, K, T), f32),
+                pltpu.VMEM((G * EL, T), i32), pltpu.VMEM((n, K, T), i32), pltpu.VMEM((G, K, T), i32), pltpu.VMEM((G, K, T), f32),
                 dma(n), dma(n), dma(n), dma(n), dma(G), dma(G), dma(G), dma(G),
                 dma(G, n), dma(G, n), dma(G, EL * n), dma(G, EL * n), dma(G), dma(G), dma(G, EL),
                 dma(G + n), dma(EL, 3), dma(1),

time: 345 us -> 340 us (0.986)
  Pallas kernels: 338 us -> 333 us
    pallas_call x1, Pallas kernels: 338 us -> 333 us  [local(): pl.pallas_call(functools.partial(_moe_kernel, G, n, EL, C, CG, T, D, F, K...]
where the time goes in v3:
time: 340 us; the launch traced here: 339 us
  Pallas kernels  333 us (98%)
  local copies, waits for them, and re-layouts  5.8 us (2%)
    pallas_call x1, Pallas kernels, local(): pl.pallas_call(functools.partial(_moe_kernel, G, n, EL, C, CG, T, D, F, K...  333 us

profile of v3, /device:TPU:98, one launch (start us, length us, event | category | flops | bytes accessed | tf_op | source)
XLA Modules:
  0.0 338.6 jit_solution(2087828755301452324)
XLA Ops:
  0.0 1.3 reshape.6
  1.3 1.3 reshape.7
  2.6 332.8 %moe.1 = (bf16[512,2048]{1,0:T(8,128)(2,1)}, bf16[8,288,2048]{2,1,0:T(8,128)(2,1)}, bf16[4,512,2048]{2,1,0:T(8,128)(2,1)}, bf16[4,8,144,2048]{3,2,1,0:T(8,128)(2...) custom-call(bf16[512,2048]{1,0:T(8,128)(2,1)} %x_ref.1, ...), custom_call_target="tpu_custom_call" | custom-call | tf_op jit(solution)/shard_map/moe/pallas_call | solution.py:462
  335.4 3.2 copy.11
